TPU v7x, 128 devices: a whole 4x4x4 slice. The times are simulated.
128 devices in a mesh: wide: 8 (over y_lo, z), narrow: 16 (over y_hi, x, core).
Axes of the slice: x: 4, y: 4 (y_hi: 2, y_lo: 2; y = y_hi * 2 + y_lo), z: 4, core: 2. Of those that a mesh axis runs over, the one named last changes fastest.
Arguments:
- saved_inputs: bfloat16 [2048, 5120], P('wide', 'narrow'), may hold values from -6 to 6
- out_grads: bfloat16 [2048, 5120], P('wide', 'narrow'), may hold values from -48 to 48
- seq_ids: int32 [2048], P('wide'), may hold values from 0 to 15, as said below
- seq_counts: int32 [16], P('wide'), may hold values from 64 to 192, as said below
- basis_in: bfloat16 [5120, 5120], P('narrow'), may hold values from -0.078125 to 0.078125
- basis_out: bfloat16 [5120, 5120], P('narrow'), may hold values from -0.078125 to 0.078125
- query_rotated: bfloat16 [5120, 5120], P('narrow', 'wide'), may hold values from -6 to 6
- damping: float32 [], replicated, may hold values from 0.05 to 0.5
Outputs:
- eigenvalues: float32 [5120, 5120], P('narrow', 'wide')
- preconditioned: float32 [5120, 5120], P('narrow', 'wide')
Inputs may be any that keep to these rules, and one draw needn't show every extreme that they name: seq_ids names for each token its sequence; the 256 tokens of block w of the token axis belong to the sequences 2 * w to 2 * w + 1, each having at least one token. seq_counts[s] is the number of tokens whose seq_ids equal s.
All inputs are finite; a program needn't handle non-finite values.
Results may differ from a plain program's by a relative error of at most 0.01.
Values may be sent and summed in bfloat16 or wider, within the bound.
A program may use at most 128 MiB of HBM per device.

v0:
```python
import jax
import jax.numpy as jnp
from jax import lax
from jax.sharding import PartitionSpec as P


def in_order(pieces, dim):
    pieces = jnp.moveaxis(pieces, 0, dim)
    shape = pieces.shape
    return pieces.reshape(*shape[:dim], shape[dim] * shape[dim + 1], *shape[dim + 2 :])


def copy_for_each(value, axis):
    copies = jnp.broadcast_to(value, (lax.axis_size(axis), *value.shape))
    return lax.all_to_all(copies, axis, split_axis=0, concat_axis=0, tiled=True)


def collect(value, axis, dim):
    return in_order(copy_for_each(value, axis), dim)


def in_one_piece(arrays, axis, dim, along):
    widths = [a.shape[along] for a in arrays]
    both = jnp.concatenate(arrays, axis=along)
    whole = lax.all_gather(both, axis, axis=dim, tiled=True)
    return tuple(jnp.split(whole, [sum(widths[:k]) for k in range(1, len(widths))], axis=along))


def shards(
    saved_inputs, out_grads, seq_ids, seq_counts, basis_in, basis_out, query_rotated, damping
):
    part_in = jnp.dot(saved_inputs, basis_in, preferred_element_type=jnp.float32)
    part_grad = jnp.dot(out_grads, basis_out, preferred_element_type=jnp.float32)
    rot_in = lax.psum(part_in, "narrow").astype(jnp.bfloat16)
    rot_grad = lax.psum_scatter(part_grad, "narrow", scatter_dimension=1, tiled=True).astype(
        jnp.bfloat16
    )
    seq_local = seq_counts.shape[0]
    tok_local = seq_ids.shape[0]
    offset = lax.axis_index("wide") * seq_local
    member = seq_ids[None, :] - offset == jnp.arange(seq_local, dtype=jnp.int32)[:, None]
    weight = (
        jnp.where(member, 1.0, 0.0).astype(jnp.float32) / seq_counts.astype(jnp.float32)[:, None]
    )
    weighted = (rot_grad.astype(jnp.float32)[None, :, :] * weight[:, :, None]).astype(jnp.bfloat16)
    total_seqs = seq_local * lax.axis_size("wide")
    groups = lax.axis_size("wide")
    all_weighted = collect(weighted, "wide", 0)
    all_weighted = all_weighted.reshape(groups, seq_local, tok_local, all_weighted.shape[2])
    column_rows = lax.all_to_all(rot_in, "wide", split_axis=1, concat_axis=0, tiled=True)
    column_rows = column_rows.reshape(groups, tok_local, column_rows.shape[1])
    per_seq = jnp.einsum(
        "gsti,gtj->gsij", all_weighted, column_rows, preferred_element_type=jnp.float32
    )
    eigenvalues = jnp.sum(per_seq * per_seq, axis=(0, 1)) / total_seqs
    scaled = (query_rotated.astype(jnp.float32) / (eigenvalues + damping)).astype(jnp.bfloat16)
    width = query_rotated.shape[1]
    in_columns = lax.dynamic_slice_in_dim(basis_in, lax.axis_index("wide") * width, width, 1)
    all_scaled, all_columns = in_one_piece((scaled, in_columns), "narrow", 0, 1)
    middle = jnp.dot(basis_out, all_scaled, preferred_element_type=jnp.float32).astype(jnp.bfloat16)
    partial_back = lax.dot_general(
        middle, all_columns, (((1,), (1,)), ((), ())), preferred_element_type=jnp.float32
    )
    preconditioned = lax.psum_scatter(partial_back, "wide", scatter_dimension=1, tiled=True)
    return (eigenvalues, preconditioned)


def solution(mesh):
    return jax.shard_map(
        shards,
        mesh=mesh,
        in_specs=(
            P("wide", "narrow"),
            P("wide", "narrow"),
            P("wide"),
            P("wide"),
            P("narrow", None),
            P("narrow", None),
            P("narrow", "wide"),
            P(),
        ),
        out_specs=(P("narrow", "wide"), P("narrow", "wide")),
        check_vma=False,
    )
```

profile of v0, /device:TPU:1, one launch (start us, length us, event | category | flops | bytes accessed | tf_op | source)
XLA Modules:
  0.0 396.9 jit_solution(1464753406761184582)
XLA Ops:
  7.2 0.0 copy-start
  7.2 0.0 reduce-scatter.3.cloned.1.call-start
  7.2 1.9 copy-done
  9.1 5.0 %fusion.11 = f32[256,5120]{0,1:T(8,128)} fusion(bf16[256,320]{0,1:T(8,128)(2,1)} %param.9, bf16[320,5120]{1,0:T(8,128)(2,1)S(1)} %copy-done), kind=kOutput, calls=%fused_computation.17 | convolution fusion | flops 838860800 | bytes 8683520 | tf_op jit(solution)/shard_map/dot_general | solution.py:33
  14.1 0.0 copy-start.3
  14.1 0.0 reduce-scatter.3.cloned.1.call-update
  14.2 0.9 copy-done.3
  15.0 5.8 %fusion.12 = f32[256,5120]{1,0:T(8,128)} fusion(bf16[256,320]{0,1:T(8,128)(2,1)S(1)} %copy-done.3, bf16[320,5120]{1,0:T(8,128)(2,1)} %param.12), kind=kOutput, calls=%fused_computation.18 | convolution fusion | flops 838860800 | bytes 8683520 | tf_op jit(solution)/shard_map/dot_general | solution.py:32
  20.9 100.9 %all-reduce.1 = bf16[256,5120]{1,0:T(8,128)(2,1)} all-reduce(f32[256,5120]{1,0:T(8,128)} %fusion.12), channel_id=1, replica_groups=mesh['wide'=8,'narrow'=16] {'narrow'}, use_global_device_ids=true, to_apply=%region_1.0 | all-reduce | flops 1310720 | bytes 7864320 | tf_op jit(solution)/shard_map/psum | solution.py:34
  121.8 3.5 copy.14
  125.3 0.0 copy-start.5
  125.3 0.0 copy-start.4
  125.3 9.7 %all-to-all-start.1 = ((bf16[256,8,640]{2,0,1:T(8,128)(2,1)}), bf16[256,8,640]{2,0,1:T(8,128)(2,1)}, u32[]{:S(2)}, u32[]{:S(2)}) async-start(bf16[256,8,640]{2,0,1:T(8,128)(2,1)} %bitcast.17), calls=%async_computation.2 | async-start | bytes 5242880 | tf_op jit(solution)/shard_map/all_to_all | solution.py:50
  135.0 0.0 copy-done.5
  135.0 0.0 copy-done.4
  135.1 0.1 fusion.10
  135.1 0.0 reduce-scatter.3.cloned.1.call-done
  135.1 1.0 convert_convert_fusion
  136.1 0.8 multiply_convert_fusion
  136.9 30.0 %all-to-all-done.1 = bf16[256,8,640]{2,0,1:T(8,128)(2,1)} async-done(((bf16[256,8,640]{2,0,1:T(8,128)(2,1)}), bf16[256,8,640]{2,0,1:T(8,128)(2,1)}, u32[]{:S(2)}, u32[]{:S(2)}) %all-to-all-start.1) | async-done | bytes 2621472 | tf_op jit(solution)/shard_map/all_to_all | solution.py:50
  167.0 2.7 broadcast_in_dim.18
  169.7 4.4 %all-to-all-start = ((bf16[8,2,256,320]{2,3,1,0:T(8,128)(2,1)}), bf16[8,2,256,320]{2,3,1,0:T(8,128)(2,1)}, u32[]{:S(2)}, u32[]{:S(2)}) async-start(bf16[8,2,256,320]{2,3,1,0:T(8,128)(2,1)} %broadcast_in_dim.18), calls=%async_computation.1 | async-start | bytes 5242880 | tf_op jit(solution)/shard_map/all_to_all | solution.py:15
  174.1 0.0 all-gather.2.cloned.1.call-start
  174.8 1.8 constant_dynamic-slice_fusion
  176.6 29.3 %all-to-all-done = bf16[8,2,256,320]{2,3,1,0:T(8,128)(2,1)} async-done(((bf16[8,2,256,320]{2,3,1,0:T(8,128)(2,1)}), bf16[8,2,256,320]{2,3,1,0:T(8,128)(2,1)}, u32[]{:S(2)}, u32[]{:S(2)}) %all-to-all-start) | async-done | bytes 2621472 | tf_op jit(solution)/shard_map/all_to_all | solution.py:15
  205.9 0.0 copy-start.2
  205.9 0.0 copy-start.1
  205.9 4.9 %multiply_reduce_fusion = f32[320,640]{1,0:T(8,128)S(1)} fusion(bf16[8,2,256,320]{2,3,1,0:T(8,128)(2,1)} %all-to-all-done, bf16[256,8,640]{2,0,1:T(8,128)(2,1)} %all-to-all-done.1), kind=kOutput, calls=%fused_computation | convolution fusion | flops 1684070400 | bytes 6062080 | tf_op jit(solution)/shard_map/gsti,gtj->gsij/dot_general | solution.py:52
  210.8 0.0 copy-done.2
  210.8 1.0 divide_convert_fusion
  211.8 0.0 copy-done.1
  211.8 1.0 pad_maximum_fusion
  212.8 0.0 all-gather.2.cloned.1.call-update
  212.8 0.2 reduce-scatter.5.cloned.1.call-start
  213.0 90.6 %all-gather.2.cloned.1.call-done = bf16[5120,1280]{1,0:T(8,128)(2,1)} async-done(((bf16[320,1280]{1,0:T(8,128)(2,1)}), bf16[5120,1280]{1,0:T(8,128)(2,1)}) %all-gather.2.cloned.1.call-update) | async-done | bytes 13107216 | tf_op jit(solution)/shard_map/all_gather | solution.py:25
  303.6 13.7 %fusion = f32[320,5120]{1,0:T(8,128)} fusion(bf16[5120,1280]{1,0:T(8,128)(2,1)} %all-gather.2.cloned.1.call-done, bf16[320,5120]{1,0:T(8,128)(2,1)S(1)} %copy-done), kind=kOutput, calls=%fused_computation.1 | convolution fusion | flops 4194508800 | bytes 22937600 | tf_op jit(solution)/shard_map/dot_general | solution.py:61
  317.3 0.0 reduce-scatter.5.cloned.1.call-update
  317.3 73.1 %reduce-scatter.5.cloned.1.call-done = f32[320,640]{1,0:T(8,128)} async-done(((f32[320,5120]{1,0:T(8,128)}), f32[320,640]{1,0:T(8,128)}) %reduce-scatter.5.cloned.1.call-update) | async-done | bytes 819216 | tf_op jit(solution)/shard_map/reduce_scatter | solution.py:64
  (2 shorter events, 0.0 us)
Async XLA Ops:
  7.2 1.9 copy-start
  7.2 128.0 %reduce-scatter.3.cloned.1.call-start = ((), (), s32[]{:S(2)}) async-start(), calls=%async_computation.4 | async-start | bytes 5570560 | tf_op jit(solution)/shard_map/reduce_scatter | solution.py:35
  14.1 0.9 copy-start.3
  125.3 9.7 %copy-start.5 = (s32[2]{0:T(128)S(1)}, s32[2]{0:T(128)}, u32[]{:S(2)}) copy-start(s32[2]{0:T(128)} %param.11) | copy-start | bytes 28
  125.3 9.7 %copy-start.4 = (s32[256]{0:T(256)S(1)}, s32[256]{0:T(256)}, u32[]{:S(2)}) copy-start(s32[256]{0:T(256)} %param.10) | copy-start | bytes 3076
  125.3 41.6 %all-to-all-start.1 = ((bf16[256,8,640]{2,0,1:T(8,128)(2,1)}), bf16[256,8,640]{2,0,1:T(8,128)(2,1)}, u32[]{:S(2)}, u32[]{:S(2)}) async-start(bf16[256,8,640]{2,0,1:T(8,128)(2,1)} %bitcast.17), calls=%async_computation.2 | async-start | bytes 5242880 | tf_op jit(solution)/shard_map/all_to_all | solution.py:50
  169.7 36.2 %all-to-all-start = ((bf16[8,2,256,320]{2,3,1,0:T(8,128)(2,1)}), bf16[8,2,256,320]{2,3,1,0:T(8,128)(2,1)}, u32[]{:S(2)}, u32[]{:S(2)}) async-start(bf16[8,2,256,320]{2,3,1,0:T(8,128)(2,1)} %broadcast_in_dim.18), calls=%async_computation.1 | async-start | bytes 5242880 | tf_op jit(solution)/shard_map/all_to_all | solution.py:15
  174.1 129.5 %all-gather.2.cloned.1.call-start = ((), (), s32[]{:S(2)}) async-start(), calls=%async_computation.5 | async-start | bytes 13926400 | tf_op jit(solution)/shard_map/all_gather | solution.py:25
  205.9 4.9 %copy-start.2 = (bf16[320,640]{1,0:T(8,128)(2,1)S(1)}, bf16[320,640]{1,0:T(8,128)(2,1)}, u32[]{:S(2)}) copy-start(bf16[320,640]{1,0:T(8,128)(2,1)} %param.14) | copy-start | bytes 1228804
  205.9 5.9 %copy-start.1 = (bf16[320,640]{1,0:T(8,128)(2,1)S(1)}, bf16[320,640]{1,0:T(8,128)(2,1)}, u32[]{:S(2)}) copy-start(bf16[320,640]{1,0:T(8,128)(2,1)} %constant_dynamic-slice_fusion) | copy-start | bytes 1228804
  212.8 177.5 %reduce-scatter.5.cloned.1.call-start = ((), (), s32[]{:S(2)}) async-start(), calls=%async_computation.6 | async-start | bytes 7372800 | tf_op jit(solution)/shard_map/reduce_scatter | solution.py:64
Sparse Core Ops, SparseCore 0:
  14.3 107.6 reduce-scatter.2
  212.9 90.6 all-gather.1
  317.4 72.8 reduce-scatter.4
where the time goes:
time: 397 us
  waiting for transfers between devices  223 us (56%)
  blocking collectives  101 us (25%)
  matrix products  29.4 us (7%)
  between operations  14.5 us (4%)
  starting transfers between devices  14.4 us (4%)
  local copies, waits for them, and re-layouts  10.9 us (3%)
    psum x1, blocking collectives, shards(): rot_in = lax.psum(part_in, 'narrow').astype(jnp.bfloat16)  101 us
    all_gather x1, waiting for transfers between devices, in_one_piece(): whole = lax.all_gather(both, axis, axis=dim, tiled=True)  90.6 us
    reduce_scatter x1, waiting for transfers between devices, shards(): lax.psum_scatter(partial_back, 'wide', scatter_dimension=1, tiled=True)  73.1 us
    all_to_all x1, waiting for transfers between devices, shards(): lax.all_to_all(rot_in, 'wide', split_axis=1, concat_axis=0, tiled=True)  30 us
    all_to_all x1, waiting for transfers between devices, copy_for_each(): return lax.all_to_all(copies, axis, split_axis=0, concat_axis=0, tiled=True)  29.3 us
    dot_general x1, matrix products, shards(): lax.dot_general(middle, all_columns, (((1,), (1,)), ((), ())), preferred_...  13.7 us
    all_to_all x1, starting transfers between devices, shards(): lax.all_to_all(rot_in, 'wide', split_axis=1, concat_axis=0, tiled=True)  9.72 us
  transfers between devices with their start and end apart: 5, of which 4 were waited for; matrix products, arithmetic and copies ran while one was open for 3% of the time, Pallas kernels for 0%

commit v1 on v0

--- a/solution.py
+++ b/solution.py
@@ -31,7 +31,8 @@
 ):
     part_in = jnp.dot(saved_inputs, basis_in, preferred_element_type=jnp.float32)
     part_grad = jnp.dot(out_grads, basis_out, preferred_element_type=jnp.float32)
-    rot_in = lax.psum(part_in, "narrow").astype(jnp.bfloat16)
+    fit_face = lambda point: jnp.sum(lax.all_gather(point, axis_name="narrow"), axis=0)
+    rot_in = fit_face(part_in).astype(jnp.bfloat16)
     rot_grad = lax.psum_scatter(part_grad, "narrow", scatter_dimension=1, tiled=True).astype(
         jnp.bfloat16
     )

time: 397 us -> 804 us (2.03)
  waiting for transfers between devices: 223 us -> 703 us
  blocking collectives: 101 us -> 0 us
  other arithmetic: 3.84 us -> 30.9 us
    all_gather x0 -> x1, waiting for transfers between devices: none -> 431 us  [shards(): lax.all_gather(point, axis_name='narrow')]
    psum x1 -> x0, blocking collectives: 101 us -> none  [shards(): rot_in = lax.psum(part_in, 'narrow').astype(jnp.bfloat16)]
    reduce_scatter x1, waiting for transfers between devices: 0.01 us -> 79.5 us  [shards(): lax.psum_scatter(part_grad, 'narrow', scatter_dimension=1, tiled=True)]
    all_to_all x1, waiting for transfers between devices: 29.3 us -> 0.01 us  [copy_for_each(): return lax.all_to_all(copies, axis, split_axis=0, concat_axis=0, tiled=True)]
    reduce_sum x0 -> x1, other arithmetic: none -> 27.8 us  [shards(): jnp.sum(lax.all_gather(point, axis_name='narrow'), axis=0)]
    convert_element_type x0 -> x2, local copies, waits for them, and re-layouts: none -> 8.76 us  [shards(): rot_in = fit_face(part_in).astype(jnp.bfloat16)]
  transfers between devices with their start and end apart: 5 -> 6, of which waited for: 4 -> 5; matrix products, arithmetic and copies ran while one was open for 3% -> 6% of each run, Pallas kernels for 0% -> 0%
where the time goes in v1:
time: 804 us; the launch traced here: 803 us
  waiting for transfers between devices  703 us (87%)
  other arithmetic  30.9 us (4%)
  matrix products  29.8 us (4%)
  local copies, waits for them, and re-layouts  15.7 us (2%)
  between operations  14.5 us (2%)
  starting transfers between devices  9.17 us (1%)
    all_gather x1, waiting for transfers between devices, shards(): lax.all_gather(point, axis_name='narrow')  431 us
    all_gather x1, waiting for transfers between devices, in_one_piece(): whole = lax.all_gather(both, axis, axis=dim, tiled=True)  89.9 us
    reduce_scatter x1, waiting for transfers between devices, shards(): lax.psum_scatter(part_grad, 'narrow', scatter_dimension=1, tiled=True)  79.5 us
    reduce_scatter x1, waiting for transfers between devices, shards(): lax.psum_scatter(partial_back, 'wide', scatter_dimension=1, tiled=True)  73.1 us
    all_to_all x1, waiting for transfers between devices, shards(): lax.all_to_all(rot_in, 'wide', split_axis=1, concat_axis=0, tiled=True)  29.4 us
    reduce_sum x1, other arithmetic, shards(): jnp.sum(lax.all_gather(point, axis_name='narrow'), axis=0)  27.8 us
  transfers between devices with their start and end apart: 6, of which 5 were waited for; matrix products, arithmetic and copies ran while one was open for 6% of the time, Pallas kernels for 0%

profile of v1, /device:TPU:1, one launch (start us, length us, event | category | flops | bytes accessed | tf_op | source)
XLA Modules:
  0.0 803.3 jit_solution(12637595323661226069)
XLA Ops:
  7.2 0.0 copy-start
  7.2 0.0 reduce-scatter.3.cloned.1.call-start
  7.2 1.9 copy-done
  9.1 5.0 fusion.11
  14.1 0.0 copy-start.3
  14.1 0.0 reduce-scatter.3.cloned.1.call-update
  14.2 0.0 all-gather.6.cloned.1.call-start
  14.2 0.8 copy-done.3
  15.0 5.8 fusion.12
  20.8 0.0 copy-start.5
  20.8 0.0 copy-start.4
  20.9 0.0 all-gather.6.cloned.1.call-update
  20.9 0.6 copy-done.5
  21.5 0.0 copy-done.4
  21.5 0.1 fusion.10
  21.6 79.5 %reduce-scatter.3.cloned.1.call-done = f32[256,320]{0,1:T(8,128)} async-done(((f32[256,5120]{0,1:T(8,128)}), f32[256,320]{0,1:T(8,128)}) %reduce-scatter.3.cloned.1.call-update) | async-done | bytes 327696 | tf_op jit(solution)/shard_map/reduce_scatter | solution.py:36
  101.1 1.0 convert_convert_fusion
  102.2 1.8 broadcast_in_dim.18
  103.9 4.4 all-to-all-start
  108.4 431.4 %all-gather.6.cloned.1.call-done = f32[4096,5120]{1,0:T(8,128)} async-done(((f32[256,5120]{1,0:T(8,128)}), f32[4096,5120]{1,0:T(8,128)}) %all-gather.6.cloned.1.call-update) | async-done | bytes 83886096 | tf_op jit(solution)/shard_map/all_gather | solution.py:34
  539.7 27.8 %reduce_sum.18 = bf16[256,5120]{1,0:T(8,128)(2,1)} reduce(f32[16,256,5120]{2,1,0:T(8,128)} %bitcast, f32[]{:T(128)} %constant.7.clone.1), dimensions={0}, to_apply=%region_1.0 | reduce | flops 19660800 | bytes 86507520 | tf_op jit(solution)/shard_map/reduce_sum | solution.py:34
  567.5 4.4 copy.11
  571.9 4.4 copy.12
  576.3 0.0 all-to-all-done
  576.3 4.4 all-to-all-start.1
  580.7 0.0 all-gather.4.cloned.1.call-start
  581.4 1.8 constant_dynamic-slice_fusion
  583.2 29.4 %all-to-all-done.1 = bf16[256,8,640]{2,0,1:T(8,128)(2,1)} async-done(((bf16[256,8,640]{2,0,1:T(8,128)(2,1)}), bf16[256,8,640]{2,0,1:T(8,128)(2,1)}, u32[]{:S(2)}, u32[]{:S(2)}) %all-to-all-start.1) | async-done | bytes 2621472 | tf_op jit(solution)/shard_map/all_to_all | solution.py:51
  612.6 0.0 copy-start.2
  612.6 0.0 copy-start.1
  612.6 4.9 multiply_reduce_fusion
  617.4 0.0 copy-done.2
  617.5 1.0 divide_convert_fusion
  618.5 0.0 copy-done.1
  618.5 1.0 pad_maximum_fusion
  619.4 0.0 all-gather.4.cloned.1.call-update
  619.5 0.2 reduce-scatter.5.cloned.1.call-start
  619.7 89.9 %all-gather.4.cloned.1.call-done = bf16[5120,1280]{1,0:T(8,128)(2,1)} async-done(((bf16[320,1280]{1,0:T(8,128)(2,1)}), bf16[5120,1280]{1,0:T(8,128)(2,1)}) %all-gather.4.cloned.1.call-update) | async-done | bytes 13107216 | tf_op jit(solution)/shard_map/all_gather | solution.py:25
  709.6 14.1 %fusion = f32[320,5120]{1,0:T(8,128)} fusion(bf16[5120,1280]{1,0:T(8,128)(2,1)} %all-gather.4.cloned.1.call-done, bf16[320,5120]{1,0:T(8,128)(2,1)S(1)} %copy-done), kind=kOutput, calls=%fused_computation.1 | convolution fusion | flops 4194508800 | bytes 22937600 | tf_op jit(solution)/shard_map/dot_general | solution.py:62
  723.7 0.0 reduce-scatter.5.cloned.1.call-update
  723.7 73.1 %reduce-scatter.5.cloned.1.call-done = f32[320,640]{1,0:T(8,128)} async-done(((f32[320,5120]{1,0:T(8,128)}), f32[320,640]{1,0:T(8,128)}) %reduce-scatter.5.cloned.1.call-update) | async-done | bytes 819216 | tf_op jit(solution)/shard_map/reduce_scatter | solution.py:65
  (3 shorter events, 0.1 us)
Async XLA Ops:
  7.2 1.9 copy-start
  7.2 93.9 %reduce-scatter.3.cloned.1.call-start = ((), (), s32[]{:S(2)}) async-start(), calls=%async_computation.4 | async-start | bytes 5570560 | tf_op jit(solution)/shard_map/reduce_scatter | solution.py:36
  14.1 0.9 copy-start.3
  14.2 525.6 %all-gather.6.cloned.1.call-start = ((), (), s32[]{:S(2)}) async-start(), calls=%async_computation.7 | async-start | bytes 89128960 | tf_op jit(solution)/shard_map/all_gather | solution.py:34
  20.8 0.7 copy-start.5
  20.8 0.7 copy-start.4
  103.9 472.3 %all-to-all-start = ((bf16[8,2,256,320]{2,3,1,0:T(8,128)(2,1)}), bf16[8,2,256,320]{2,3,1,0:T(8,128)(2,1)}, u32[]{:S(2)}, u32[]{:S(2)}) async-start(bf16[8,2,256,320]{2,3,1,0:T(8,128)(2,1)} %broadcast_in_dim.18), calls=%async_computation.1 | async-start | bytes 5242880 | tf_op jit(solution)/shard_map/all_to_all | solution.py:15
  576.3 36.3 %all-to-all-start.1 = ((bf16[256,8,640]{2,0,1:T(8,128)(2,1)}), bf16[256,8,640]{2,0,1:T(8,128)(2,1)}, u32[]{:S(2)}, u32[]{:S(2)}) async-start(bf16[256,8,640]{2,0,1:T(8,128)(2,1)} %copy.12), calls=%async_computation.2 | async-start | bytes 5242880 | tf_op jit(solution)/shard_map/all_to_all | solution.py:51
  580.7 128.9 %all-gather.4.cloned.1.call-start = ((), (), s32[]{:S(2)}) async-start(), calls=%async_computation.5 | async-start | bytes 13926400 | tf_op jit(solution)/shard_map/all_gather | solution.py:25
  612.6 4.9 copy-start.2
  612.6 5.9 copy-start.1
  619.5 177.3 %reduce-scatter.5.cloned.1.call-start = ((), (), s32[]{:S(2)}) async-start(), calls=%async_computation.6 | async-start | bytes 7372800 | tf_op jit(solution)/shard_map/reduce_scatter | solution.py:65
Sparse Core Ops, SparseCore 0:
  14.3 86.8 reduce-scatter.2
  103.6 436.0 all-gather.5
  619.6 89.9 all-gather.3
  723.8 72.8 reduce-scatter.4
